TPU v7x, 32 devices: a whole 2x2x4 slice. The times are simulated.
32 devices in a mesh: dp: 4 (over x, core), seq: 2 (over y), mp: 4 (over z).
Axes of the slice: x: 2, y: 2, z: 4, core: 2. Of those that a mesh axis runs over, the one named last changes fastest.
Arguments:
- inputs: bfloat16 [6272, 1024], P(('dp', 'seq', 'mp')), may hold values from -6 to 6
- grad_out: bfloat16 [6272, 1024], P(('dp', 'seq', 'mp')), may hold values from -6 to 6
- pad_mask: int32 [6272], P(('dp', 'seq', 'mp')), may hold values from 0 to 1, as said below
- hidden_pre: bfloat16 [6272, 4096], P(('dp', 'seq'), 'mp'), may hold values from -6 to 6
- w_in: bfloat16 [1024, 4096], P(None, 'mp'), may hold values from -0.1875 to 0.1875
- w_out: bfloat16 [4096, 1024], P('mp'), may hold values from -0.09375 to 0.09375
- ln_gain: float32 [1024], replicated, may hold values from 0.25 to 1.75
- ln_shift: float32 [1024], replicated, may hold values from -3 to 3
Outputs:
- grad_inputs: bfloat16 [6272, 1024], P(('dp', 'seq', 'mp'))
- grad_w_in: float32 [1024, 4096], P('seq', 'mp')
- grad_w_out: float32 [4096, 1024], P('mp', 'seq')
Inputs may be any that keep to these rules, and one draw needn't show every extreme that they name: `pad_mask`: each window is 196 consecutive tokens, 14 rows of 14 in row order; its image tokens are those in its first h rows and first w columns, h and w between 4 and 14; some windows are full and some are not in every draw.
All inputs are finite; a program needn't handle non-finite values.
Results may differ from a plain program's by a relative error of at most 0.02.
Values may be sent and summed in bfloat16 or wider, within the bound.
A program may use at most 64 MiB of HBM per device.

v0:
```python
import jax
import jax.numpy as jnp
from jax import lax
from jax.sharding import PartitionSpec as P

EPSILON = 1e-06
ROOT_HALF = 0.7071067811865476
INV_ROOT_TAU = 0.3989422804014327


def gelu_pair(hidden_pre):
    values = hidden_pre.astype(jnp.float32)
    normal_cdf = 0.5 * (1.0 + lax.erf(values * ROOT_HALF))
    normal_pdf = jnp.exp(-0.5 * values * values) * INV_ROOT_TAU
    return (values * normal_cdf, normal_cdf + values * normal_pdf)


def shards(inputs, grad_out, pad_mask, hidden_pre, w_in, w_out, ln_gain, ln_shift):
    own_rows = inputs.shape[0]
    values = inputs.astype(jnp.float32)
    row_mean = jnp.mean(values, axis=1, keepdims=True)
    centred = values - row_mean
    row_var = jnp.mean(centred * centred, axis=1, keepdims=True)
    inv_std = lax.rsqrt(row_var + EPSILON)
    x_hat = centred * inv_std
    normed = (x_hat * ln_gain + ln_shift).astype(jnp.bfloat16)
    masked = (grad_out.astype(jnp.float32) * pad_mask.astype(jnp.float32)[:, None]).astype(
        jnp.bfloat16
    )
    normed_all, masked_all = (
        lax.all_gather(normed, "mp", axis=0, tiled=True),
        lax.all_gather(masked, "mp", axis=0, tiled=True),
    )
    activation, slope = gelu_pair(hidden_pre)
    activation = activation.astype(jnp.bfloat16)
    d_act = jnp.dot(masked_all, w_out.T, preferred_element_type=jnp.float32)
    d_hidden = (d_act * slope).astype(jnp.bfloat16)
    term_out = jnp.dot(activation.T, masked_all, preferred_element_type=jnp.float32)
    term_in = jnp.dot(normed_all.T, d_hidden, preferred_element_type=jnp.float32)
    d_normed = lax.psum_scatter(
        jnp.dot(d_hidden, w_in.T, preferred_element_type=jnp.float32).astype(jnp.bfloat16),
        "mp",
        scatter_dimension=0,
        tiled=True,
    ).astype(jnp.float32)
    d_hat = d_normed * ln_gain
    first_term = jnp.mean(d_hat, axis=1, keepdims=True)
    second_term = jnp.mean(d_hat * x_hat, axis=1, keepdims=True)
    grad_inputs = (
        masked.astype(jnp.float32) + inv_std * (d_hat - first_term - x_hat * second_term)
    ).astype(jnp.bfloat16)
    piece_in, piece_out = (
        lax.psum_scatter(
            term_in.astype(jnp.bfloat16), "seq", scatter_dimension=0, tiled=True
        ).astype(jnp.float32),
        lax.psum_scatter(
            term_out.astype(jnp.bfloat16), "seq", scatter_dimension=1, tiled=True
        ).astype(jnp.float32),
    )
    piece_in, piece_out = (
        lax.psum(piece_in.astype(jnp.bfloat16), "dp").astype(jnp.float32),
        lax.psum(piece_out.astype(jnp.bfloat16), "dp").astype(jnp.float32),
    )
    token_total = own_rows * lax.axis_size("dp") * lax.axis_size("seq") * lax.axis_size("mp")
    scale = float(token_total) ** (-0.5)
    return (grad_inputs, piece_in * scale, piece_out * scale)


def solution(mesh):
    return jax.shard_map(
        shards,
        mesh=mesh,
        in_specs=(
            P(("dp", "seq", "mp"), None),
            P(("dp", "seq", "mp"), None),
            P(("dp", "seq", "mp")),
            P(("dp", "seq"), "mp"),
            P(None, "mp"),
            P("mp", None),
            P(),
            P(),
        ),
        out_specs=(P(("dp", "seq", "mp"), None), P("seq", "mp"), P("mp", "seq")),
        check_vma=False,
    )
```

profile of v0, /device:TPU:0, one launch (start us, length us, event | category | flops | bytes accessed | tf_op | source)
XLA Modules:
  0.0 274.8 jit_solution(7448456455352834533)
XLA Ops:
  7.2 0.8 convert_element_type.53
  8.0 1.9 fusion.26
  10.0 1.1 convert_reduce_fusion
  11.2 1.3 fusion.23
  12.4 38.6 %all-gather.5.cloned.1.call-done = bf16[4,196,1024]{2,1,0:T(8,128)(2,1)} async-done(((bf16[1,196,1024]{2,1,0:T(8,128)(2,1)}), bf16[4,196,1024]{2,1,0:T(8,128)(2,1)}) %all-gather.5.cloned.1.call-update) | async-done | bytes 1605648 | tf_op jit(solution)/shard_map/all_gather | solution.py:32
  51.0 2.5 reshape.30
  53.5 4.8 %fusion.8 = bf16[784,1024]{1,0:T(8,128)(2,1)S(1)} fusion(bf16[784,1024]{1,0:T(8,128)(2,1)} %param.11, bf16[784,1024]{1,0:T(8,128)(2,1)} %reshape.30, bf16[1024,1024]{1,0:T(8,128)(2,1)S(1)} %copy-done), kind=kOutput, calls=%fused_computation.12 | convolution fusion | flops 1652998144 | bytes 6914048 | tf_op jit(solution)/shard_map/dot_general | solution.py:36
  58.2 1.2 copy-done.7
  59.4 3.0 %convolution_convert_fusion.2 = bf16[784,1024]{1,0:T(8,128)(2,1)} fusion(bf16[784,1024]{1,0:T(8,128)(2,1)S(1)} %fusion.8, bf16[1024,1024]{1,0:T(8,128)(2,1)S(1)} %copy-done.6), kind=kOutput, calls=%fused_computation.18 | convolution fusion | flops 1644969984 | bytes 5308416 | tf_op jit(solution)/shard_map/dot_general | solution.py:41
  62.4 34.3 %fusion = bf16[200,1024]{1,0:T(8,128)(2,1)S(1)} fusion(bf16[784,1024]{1,0:T(8,128)(2,1)} %convolution_convert_fusion.2), kind=kCustom, calls=%all-reduce-scatter | all-reduce-scatter fusion | flops 819201 | bytes 2015744
  96.7 1.6 collective-permute-start
  98.4 0.6 dynamic-slice.4
  99.9 0.6 concatenate
  100.5 0.4 fusion.24
  101.0 2.4 fusion.25
  103.4 5.7 %convolution_convert_fusion = bf16[1024,1024]{1,0:T(8,128)(2,1)} fusion(bf16[784,1024]{1,0:T(8,128)(2,1)} %reshape.30, bf16[784,1024]{1,0:T(8,128)(2,1)} %param.11), kind=kOutput, calls=%fused_computation.16 | convolution fusion | flops 1650032640 | bytes 5308416 | tf_op jit(solution)/shard_map/dot_general | solution.py:38
  109.2 32.6 %all-gather.7.cloned.1.call-done = bf16[4,196,1024]{2,1,0:T(8,128)(2,1)} async-done(((bf16[1,196,1024]{2,1,0:T(8,128)(2,1)}), bf16[4,196,1024]{2,1,0:T(8,128)(2,1)}) %all-gather.7.cloned.1.call-update) | async-done | bytes 1605648 | tf_op jit(solution)/shard_map/all_gather | solution.py:31
  141.8 2.5 reshape.32
  144.2 5.6 %convolution_convert_fusion.1 = bf16[1024,1024]{1,0:T(8,128)(2,1)} fusion(bf16[784,1024]{1,0:T(8,128)(2,1)} %reshape.32, bf16[784,1024]{1,0:T(8,128)(2,1)} %copy-done.7), kind=kOutput, calls=%fused_computation.17 | convolution fusion | flops 1645215744 | bytes 5308416 | tf_op jit(solution)/shard_map/dot_general | solution.py:39
  149.9 25.5 %reduce-scatter.7.cloned.1.call-done = bf16[1024,512]{1,0:T(8,128)(2,1)} async-done(((bf16[1024,1024]{1,0:T(8,128)(2,1)}), bf16[1024,512]{1,0:T(8,128)(2,1)}) %reduce-scatter.7.cloned.1.call-update) | async-done | bytes 1048592 | tf_op jit(solution)/shard_map/reduce_scatter | solution.py:56
  175.4 34.6 %reduce-scatter.5.cloned.1.call-done = bf16[512,1024]{1,0:T(8,128)(2,1)} async-done(((bf16[1024,1024]{1,0:T(8,128)(2,1)}), bf16[512,1024]{1,0:T(8,128)(2,1)}) %reduce-scatter.5.cloned.1.call-update) | async-done | bytes 1048592 | tf_op jit(solution)/shard_map/reduce_scatter | solution.py:53
  210.0 53.7 %all-reduce.5.cloned.1.call-done = (bf16[512,1024]{1,0:T(8,128)(2,1)}, bf16[1024,512]{1,0:T(8,128)(2,1)}) async-done(((bf16[512,1024]{1,0:T(8,128)(2,1)}, bf16[1024,512]{1,0:T(8,128)(2,1)}), (bf16[512,1024]{1,0:T(8,128)(2,1)}, bf16[1024,512]{1,0:T(8,128)(2,1)})) %all-reduce.5.cloned.1.call-update) | async-done | bytes 2097168 | tf_op jit(solution)/shard_map/psum | solution.py:61
  263.7 2.9 %convert_multiply_fusion.6 = f32[512,1024]{1,0:T(8,128)} fusion(bf16[512,1024]{1,0:T(8,128)(2,1)} %get-tuple-element.5), kind=kLoop, calls=%fused_computation.15 | loop fusion | flops 1048576 | bytes 3145728 | tf_op jit(solution)/shard_map/mul | solution.py:66
  266.6 1.6 convert_multiply_fusion.5
  (30 shorter events, 0.7 us)
Async XLA Ops:
  7.2 46.3 %copy-start = (bf16[1024,1024]{1,0:T(8,128)(2,1)S(1)}, bf16[1024,1024]{1,0:T(8,128)(2,1)}, u32[]{:S(2)}) copy-start(bf16[1024,1024]{1,0:T(8,128)(2,1)} %param.13) | copy-start | bytes 6291460
  7.2 43.8 %all-gather.5.cloned.1.call-start = ((), (), s32[]{:S(2)}) async-start(), calls=%async_computation.4 | async-start | bytes 2048000 | tf_op jit(solution)/shard_map/all_gather | solution.py:32
  10.0 131.8 %all-gather.7.cloned.1.call-start = ((), (), s32[]{:S(2)}) async-start(), calls=%async_computation.5 | async-start | bytes 2048000 | tf_op jit(solution)/shard_map/all_gather | solution.py:31
  53.4 5.9 %copy-start.6 = (bf16[1024,1024]{1,0:T(8,128)(2,1)S(1)}, bf16[1024,1024]{1,0:T(8,128)(2,1)}, u32[]{:S(2)}) copy-start(bf16[1024,1024]{1,0:T(8,128)(2,1)} %param.12) | copy-start | bytes 6291460
  58.2 1.2 copy-start.7
  59.4 39.0 %copy-start.5 = (u32[32]{0:T(128)S(1)}, u32[32]{0:T(128)}, u32[]{:S(2)}) copy-start(u32[32]{0:T(128)} %constant.28) | copy-start | bytes 388
  62.4 38.1 %copy-start.1 = (bf16[196,1024]{1,0:T(8,128)(2,1)S(1)}, bf16[196,1024]{1,0:T(8,128)(2,1)}, u32[]{:S(2)}) copy-start(bf16[196,1024]{1,0:T(8,128)(2,1)} %param.8) | copy-start | bytes 1204228
  62.4 38.1 %copy-start.3 = (f32[1024]{0:T(1024)S(1)}, f32[1024]{0:T(1024)}, u32[]{:S(2)}) copy-start(f32[1024]{0:T(1024)} %param.14) | copy-start | bytes 12292
  62.4 38.5 %copy-start.4 = (f32[1024]{0:T(1024)S(1)}, f32[1024]{0:T(1024)}, u32[]{:S(2)}) copy-start(f32[1024]{0:T(1024)} %param.15) | copy-start | bytes 12292
  96.7 3.2 %collective-permute-start = (bf16[12,1024]{1,0:T(8,128)(2,1)S(1)}, bf16[12,1024]{1,0:T(8,128)(2,1)S(1)}, u32[]{:S(2)}, u32[]{:S(2)}) collective-permute-start(bf16[12,1024]{1,0:T(8,128)(2,1)S(1)} %slice), channel_id=1, source_target_pairs={{0,1},{1,2},{2,3},{4,5},{5,6},{6,7},{8,9},{9,10},{10,11},{12,13},{... | collective-permute-start | bytes 73736
  103.4 72.0 %reduce-scatter.7.cloned.1.call-start = ((), (), s32[]{:S(2)}) async-start(), calls=%async_computation.3 | async-start | bytes 3145728 | tf_op jit(solution)/shard_map/reduce_scatter | solution.py:56
  109.1 100.9 %reduce-scatter.5.cloned.1.call-start = ((), (), s32[]{:S(2)}) async-start(), calls=%async_computation.2 | async-start | bytes 3145728 | tf_op jit(solution)/shard_map/reduce_scatter | solution.py:53
  149.9 113.9 %all-reduce.5.cloned.1.call-start = ((), (), s32[]{:S(2)}) async-start(), calls=%async_computation.6 | async-start | bytes 4194304 | tf_op jit(solution)/shard_map/psum | solution.py:61
  263.7 2.9 %copy-start.2 = (bf16[1024,512]{1,0:T(8,128)(2,1)S(1)}, bf16[1024,512]{1,0:T(8,128)(2,1)}, u32[]{:S(2)}) copy-start(bf16[1024,512]{1,0:T(8,128)(2,1)} %get-tuple-element.6) | copy-start | bytes 3145732
Sparse Core Ops, SparseCore 0:
  10.1 40.8 all-gather.4
  103.5 38.2 all-gather.6
  144.6 30.7 reduce-scatter.6
  178.0 31.8 reduce-scatter.4
  212.3 51.4 all-reduce.4
where the time goes:
time: 275 us
  waiting for transfers between devices  185 us (67%)
  blocking collectives  34.3 us (12%)
  matrix products  19.1 us (7%)
  between operations  14.5 us (5%)
  other arithmetic  12.5 us (5%)
  local copies, waits for them, and re-layouts  7.29 us (3%)
    psum x1, waiting for transfers between devices, shards(): lax.psum(piece_in.astype(jnp.bfloat16), 'dp').astype(jnp.float32)  53.7 us
    all_gather x1, waiting for transfers between devices, shards(): lax.all_gather(masked, 'mp', axis=0, tiled=True)  38.6 us
    reduce_scatter x1, waiting for transfers between devices, shards(): lax.psum_scatter(term_in.astype(jnp.bfloat16), 'seq', scatter_dimension=0...  34.6 us
    unnamed x1, blocking collectives  34.3 us
    all_gather x1, waiting for transfers between devices, shards(): lax.all_gather(normed, 'mp', axis=0, tiled=True)  32.6 us
    reduce_scatter x1, waiting for transfers between devices, shards(): lax.psum_scatter(term_out.astype(jnp.bfloat16), 'seq', scatter_dimension=...  25.5 us
    unnamed x21, local copies, waits for them, and re-layouts  7.29 us
    dot_general x1, matrix products, shards(): jnp.dot(activation.T, masked_all, preferred_element_type=jnp.float32)  5.67 us
  transfers between devices with their start and end apart: 6, of which 6 were waited for; matrix products, arithmetic and copies ran while one was open for 6% of the time, Pallas kernels for 0%

commit v1 on v0

--- a/solution.py
+++ b/solution.py
@@ -1,11 +1,352 @@
+import functools
+
 import jax
 import jax.numpy as jnp
 from jax import lax
+from jax.experimental import pallas as pl
+from jax.experimental.pallas import tpu as pltpu
 from jax.sharding import PartitionSpec as P
 
 EPSILON = 1e-06
 ROOT_HALF = 0.7071067811865476
 INV_ROOT_TAU = 0.3989422804014327
+MESH = pl.DeviceIdType.MESH
+CHUNKS = 2
+BF = jnp.bfloat16
+F32 = jnp.float32
+
+
+def kernel(n, x_ref, normed_ref, masked_ref, h_ref, w_in_ref, w_out_ref, gain_ref,
+           gi_ref, out_in, out_out,
+           m_all, n_all, act, dh, dn, from_left, from_right,
+           t_in, t_out, rc_in, rc_out, ry_in, ry_out, rx_in, rx_out,
+           m_send, m_recv, n_send, n_recv, r_send, r_recv, d_send, d_recv):
+    dp, y, z = lax.axis_index("dp"), lax.axis_index("seq"), lax.axis_index("mp")
+    core = lax.rem(dp, 2)
+    half = dp // 2
+    core_peer = dp + 1 - 2 * core
+    x_peer = core + 2 * (1 - half)
+    width, ff = w_in_ref.shape
+    own_rows = normed_ref.shape[0]
+
+    has = (z < n - 1, z > 0)
+    peer = (lax.min(z + 1, n - 1), lax.max(z - 1, 0))
+
+    barrier = pltpu.get_barrier_semaphore()
+    for d in (0, 1):
+        @pl.when(has[d])
+        def _(d=d):
+            pl.semaphore_signal(barrier, inc=1, device_id={"mp": peer[d]}, device_id_type=MESH)
+    pl.semaphore_signal(barrier, inc=1, device_id={"dp": core_peer}, device_id_type=MESH)
+    pl.semaphore_signal(barrier, inc=1, device_id={"dp": x_peer}, device_id_type=MESH)
+    pl.semaphore_signal(barrier, inc=1, device_id={"seq": 1 - y}, device_id_type=MESH)
+    pl.semaphore_wait(barrier, 3 + jnp.where(z < n - 1, 1, 0) + jnp.where(z > 0, 1, 0))
+
+    def origin(d, s):
+        return z - s if d == 0 else z + s
+
+    def arrives(d, s):
+        return z >= s if d == 0 else z + s < n
+
+    def gather_copy(own, all_ref, send, recv, d, s):
+        t = jnp.clip(origin(d, s), 0, n - 1)
+        return pltpu.make_async_remote_copy(
+            src_ref=own if s == 0 else all_ref.at[t], dst_ref=all_ref.at[t],
+            send_sem=send.at[d, s], recv_sem=recv.at[d, s],
+            device_id={"mp": peer[d]}, device_id_type=MESH)
+
+    def landed(all_ref, send, recv, d, s):
+        t = jnp.clip(origin(d, s), 0, n - 1)
+        return pltpu.make_async_remote_copy(
+            src_ref=all_ref.at[t], dst_ref=all_ref.at[t],
+            send_sem=send.at[d, s - 1], recv_sem=recv.at[d, s - 1],
+            device_id={"mp": peer[d]}, device_id_type=MESH)
+
+    def m_copy(d, s):
+        return gather_copy(masked_ref, m_all, m_send, m_recv, d, s)
+
+    def n_copy(d, s):
+        return gather_copy(normed_ref, n_all, n_send, n_recv, d, s)
+
+    def forwards(d, s):
+        return jnp.logical_and(has[d], arrives(d, s))
+
+    def start_own_normed(s):
+        for d, last in ((0, z), (1, n - 1 - z)):
+            @pl.when(jnp.logical_and(has[d], last == s))
+            def _(d=d):
+                n_copy(d, 0).start()
+
+    step = 256
+
+    def process(t):
+        def body(c, carry):
+            cols = pl.ds(pl.multiple_of(c * step, step), step)
+            h = h_ref[t, :, cols].astype(F32)
+            cdf = 0.5 * (1.0 + lax.erf(h * ROOT_HALF))
+            pdf = jnp.exp(-0.5 * h * h) * INV_ROOT_TAU
+            act[t, :, cols] = (h * cdf).astype(BF)
+            d_act = lax.dot_general(m_all[t], w_out_ref[cols, :], (((1,), (1,)), ((), ())),
+                                    preferred_element_type=F32)
+            dh[t, :, cols] = (d_act * (cdf + h * pdf)).astype(BF)
+            return carry
+        lax.fori_loop(0, ff // step, body, 0)
+
+    for d in (0, 1):
+        @pl.when(has[d])
+        def _(d=d):
+            m_copy(d, 0).start()
+    start_own_normed(0)
+    m_all[z] = masked_ref[...]
+    n_all[z] = normed_ref[...]
+    process(z)
+    for s in range(1, n):
+        for d in (0, 1):
+            @pl.when(arrives(d, s))
+            def _(d=d):
+                landed(m_all, m_send, m_recv, d, s).wait_recv()
+
+            @pl.when(forwards(d, s))
+            def _(d=d):
+                m_copy(d, s).start()
+        start_own_normed(s)
+        for d in (0, 1):
+            @pl.when(arrives(d, s))
+            def _(d=d):
+                process(origin(d, s))
+
+    def back(t, carry):
+        def body(c, inner):
+            cols = pl.ds(pl.multiple_of(c * step, step), step)
+            dn[t, :, cols] = lax.dot_general(
+                dh[t], w_in_ref[cols, :], (((1,), (1,)), ((), ())),
+                preferred_element_type=F32).astype(BF)
+            return inner
+        return lax.fori_loop(0, width // step, body, carry)
+    lax.fori_loop(0, n, back, 0)
+
+    slots = (from_left, from_right)
+
+    def run_copy(d, j):
+        t = n - 1 - j if d == 0 else j
+        return pltpu.make_async_remote_copy(
+            src_ref=dn.at[t], dst_ref=slots[d].at[t],
+            send_sem=r_send.at[d, j], recv_sem=r_recv.at[d, j],
+            device_id={"mp": peer[d]}, device_id_type=MESH)
+
+    def running(j):
+        for d in (0, 1):
+            t = n - 1 - j if d == 0 else j
+            beyond = z < t if d == 0 else z > t
+            gets = jnp.logical_and(has[1 - d], z <= t if d == 0 else z >= t)
+
+            @pl.when(gets)
+            def _(d=d, t=t, j=j):
+                run_copy(d, j).wait_recv()
+
+            @pl.when(jnp.logical_and(gets, beyond))
+            def _(d=d, t=t, j=j):
+                dn[t] = (dn[t].astype(F32) + slots[d][t].astype(F32)).astype(BF)
+
+            @pl.when(beyond)
+            def _(d=d, t=t, j=j):
+                run_copy(d, j).start()
+
+    def grad_parts(which):
+        return ((t_in, rc_in, ry_in, rx_in, out_in), (t_out, rc_out, ry_out, rx_out, out_out))[which]
+
+    def d_copy(which, stage, c):
+        term, rc, ry, rx, out = grad_parts(which)
+        src, dst, target = (
+            (term.at[1 - core, c], rc.at[c], {"dp": core_peer}),
+            (term.at[core, c, 1 - y], ry.at[c], {"seq": 1 - y}),
+            (term.at[core, c, y], rx.at[c], {"dp": x_peer}),
+            (out.at[core, c], out.at[core, c], {"dp": core_peer}),
+        )[stage]
+        return pltpu.make_async_remote_copy(
+            src_ref=src, dst_ref=dst, send_sem=d_send.at[which, stage, c],
+            recv_sem=d_recv.at[which, stage, c], device_id=target, device_id_type=MESH)
+
+    def tn(lhs, rhs):
+        return lax.dot_general(lhs, rhs, (((0,), (0,)), ((), ())), preferred_element_type=F32)
+
+    rows_all = n * own_rows
+    r_out, c_out = t_out.shape[3], t_out.shape[4]
+    r_in = t_in.shape[3]
+
+    def make_out():
+        for c in range(CHUNKS):
+            def body(i, carry):
+                k = lax.rem(core + 1 + i, 2)
+                cols = pl.ds(pl.multiple_of((k * CHUNKS + c) * r_out, r_out), r_out)
+                total = tn(act[:, :, cols].reshape(rows_all, r_out),
+                           m_all[...].reshape(rows_all, width)).astype(BF)
+                for s in range(2):
+                    t_out[k, c, s] = total[:, s * c_out:(s + 1) * c_out]
+                return carry
+            lax.fori_loop(0, 2, body, 0)
+            d_copy(1, 0, c).start()
+
+    def make_in():
+        for c in range(CHUNKS):
+            def body(i, carry):
+                k = lax.rem(core + 1 + i // 2, 2)
+                s = lax.rem(i, 2)
+                cols = pl.ds(pl.multiple_of(((s * 2 + k) * CHUNKS + c) * r_in, r_in), r_in)
+                t_in[k, c, s] = tn(n_all[:, :, cols].reshape(rows_all, r_in),
+                                   dh[...].reshape(rows_all, ff)).astype(BF)
+                return carry
+            lax.fori_loop(0, 4, body, 0)
+            d_copy(0, 0, c).start()
+
+    def after_core(which):
+        term, rc, ry, rx, out = grad_parts(which)
+        for c in range(CHUNKS):
+            d_copy(which, 0, c).wait_recv()
+            for s in (1 - y, y):
+                term[core, c, s] = (term[core, c, s].astype(F32) + rc[c, s].astype(F32)).astype(BF)
+            d_copy(which, 1, c).start()
+
+    def after_seq(which):
+        term, rc, ry, rx, out = grad_parts(which)
+        for c in range(CHUNKS):
+            d_copy(which, 1, c).wait_recv()
+            term[core, c, y] = (term[core, c, y].astype(F32) + ry[c].astype(F32)).astype(BF)
+            d_copy(which, 2, c).start()
+
+    def after_chip(which):
+        term, rc, ry, rx, out = grad_parts(which)
+        for c in range(CHUNKS):
+            d_copy(which, 2, c).wait_recv()
+            out[core, c] = (term[core, c, y].astype(F32) + rx[c].astype(F32)).astype(BF)
+            d_copy(which, 3, c).start()
+
+    stages = [after_core, after_seq, after_chip]
+    make_out()
+    stages.pop(0)(1)
+    for s in range(1, n):
+        for d in (0, 1):
+            @pl.when(arrives(d, s))
+            def _(d=d):
+                landed(n_all, n_send, n_recv, d, s).wait_recv()
+
+            @pl.when(forwards(d, s))
+            def _(d=d):
+                n_copy(d, s).start()
+        running(s - 1)
+        if stages:
+            stages.pop(0)(1)
+    for stage in stages:
+        stage(1)
+    make_in()
+    after_core(0)
+    running(n - 1)
+
+    def norm_rows(i, carry):
+        rows = pl.ds(pl.multiple_of(i * 16, 16), 16)
+        values = x_ref[rows, :].astype(F32)
+        row_mean = jnp.mean(values, axis=1, keepdims=True)
+        centred = values - row_mean
+        row_var = jnp.mean(centred * centred, axis=1, keepdims=True)
+        inv_std = lax.rsqrt(row_var + EPSILON)
+        x_hat = centred * inv_std
+        total = dn[z, rows, :].astype(F32)
+        left = from_left[z, rows, :].astype(F32)
+        right = from_right[z, rows, :].astype(F32)
+        total = total + jnp.where(z > 0, left, 0.0) + jnp.where(z < n - 1, right, 0.0)
+        d_hat = total * gain_ref[...]
+        first = jnp.mean(d_hat, axis=1, keepdims=True)
+        second = jnp.mean(d_hat * x_hat, axis=1, keepdims=True)
+        gi_ref[rows, :] = (masked_ref[rows, :].astype(F32)
+                           + inv_std * (d_hat - first - x_hat * second)).astype(BF)
+        return carry
+
+    @pl.when(z == 0)
+    def _():
+        from_left[z] = jnp.zeros(from_left.shape[1:], BF)
+
+    @pl.when(z == n - 1)
+    def _():
+        from_right[z] = jnp.zeros(from_right.shape[1:], BF)
+    lax.fori_loop(0, own_rows // 16, norm_rows, 0)
+
+    after_seq(0)
+    after_chip(0)
+    for which in (1, 0):
+        for c in range(CHUNKS):
+            term, rc, ry, rx, out = grad_parts(which)
+            pltpu.make_async_remote_copy(
+                src_ref=out.at[1 - core, c], dst_ref=out.at[1 - core, c],
+                send_sem=d_send.at[which, 3, c], recv_sem=d_recv.at[which, 3, c],
+                device_id={"dp": core_peer}, device_id_type=MESH).wait_recv()
+    for which in (1, 0):
+        for stage in range(4):
+            for c in range(CHUNKS):
+                d_copy(which, stage, c).wait_send()
+    for s in range(n - 1):
+        for d in (0, 1):
+            @pl.when(forwards(d, s))
+            def _(d=d, s=s):
+                m_copy(d, s).wait_send()
+                n_copy(d, s).wait_send()
+    for j in range(n):
+        for d in (0, 1):
+            t = n - 1 - j if d == 0 else j
+
+            @pl.when(z < t if d == 0 else z > t)
+            def _(d=d, j=j):
+                run_copy(d, j).wait_send()
+
+
+def shards(n, inputs, grad_out, pad_mask, hidden_pre, w_in, w_out, ln_gain, ln_shift):
+    own_rows, width = inputs.shape
+    ff = w_in.shape[1]
+    padded = -(-own_rows // 16) * 16
+    grow = ((0, padded - own_rows), (0, 0))
+    x = jnp.pad(inputs, grow)
+    values = x.astype(F32)
+    row_mean = jnp.mean(values, axis=1, keepdims=True)
+    centred = values - row_mean
+    row_var = jnp.mean(centred * centred, axis=1, keepdims=True)
+    inv_std = lax.rsqrt(row_var + EPSILON)
+    normed = (centred * inv_std * ln_gain + ln_shift).astype(BF)
+    masked = jnp.pad((grad_out.astype(F32) * pad_mask.astype(F32)[:, None]).astype(BF), grow)
+    h = jnp.pad(hidden_pre.reshape(n, own_rows, ff), ((0, 0),) + grow)
+    in_piece = (width // (4 * CHUNKS), ff)
+    out_piece = (ff // (2 * CHUNKS), width // 2)
+    block = (n, padded, width)
+    scratch = [
+        pltpu.VMEM(block, BF), pltpu.VMEM(block, BF),
+        pltpu.VMEM((n, padded, ff), BF), pltpu.VMEM((n, padded, ff), BF),
+        pltpu.VMEM(block, BF), pltpu.VMEM(block, BF), pltpu.VMEM(block, BF),
+    ]
+    scratch += [pltpu.VMEM((2, CHUNKS, 2) + p, BF) for p in (in_piece, out_piece)]
+    scratch += [pltpu.VMEM((CHUNKS, 2) + p, BF) for p in (in_piece, out_piece)]
+    scratch += [pltpu.VMEM((CHUNKS,) + p, BF) for p in (in_piece, out_piece)] * 2
+    scratch += [pltpu.SemaphoreType.DMA((2, n))] * 6
+    scratch += [pltpu.SemaphoreType.DMA((2, 4, CHUNKS))] * 2
+    vmem = pl.BlockSpec(memory_space=pltpu.VMEM)
+    gi, g_in, g_out = pl.pallas_call(
+        functools.partial(kernel, n),
+        out_shape=(
+            jax.ShapeDtypeStruct((padded, width), BF),
+            jax.ShapeDtypeStruct((2, CHUNKS) + in_piece, BF),
+            jax.ShapeDtypeStruct((2, CHUNKS) + out_piece, BF),
+        ),
+        in_specs=[vmem] * 7,
+        out_specs=(vmem,) * 3,
+        scratch_shapes=scratch,
+        name="mlp_backward",
+        compiler_params=pltpu.CompilerParams(
+            collective_id=0, has_side_effects=True, vmem_limit_bytes=60 * 1024 * 1024),
+    )(x, normed, masked, h, w_in, w_out, ln_gain.reshape(1, width))
+    token_total = own_rows * lax.axis_size("dp") * lax.axis_size("seq") * n
+    scale = float(token_total) ** (-0.5)
+    return (
+        gi[:own_rows],
+        g_in.reshape(width // 2, ff).astype(F32) * scale,
+        g_out.reshape(ff, width // 2).astype(F32) * scale,
+    )
 
 
 def gelu_pair(hidden_pre):
@@ -15,7 +356,7 @@
     return (values * normal_cdf, normal_cdf + values * normal_pdf)
 
 
-def shards(inputs, grad_out, pad_mask, hidden_pre, w_in, w_out, ln_gain, ln_shift):
+def plain_shards(inputs, grad_out, pad_mask, hidden_pre, w_in, w_out, ln_gain, ln_shift):
     own_rows = inputs.shape[0]
     values = inputs.astype(jnp.float32)
     row_mean = jnp.mean(values, axis=1, keepdims=True)
@@ -67,8 +408,10 @@
 
 
 def solution(mesh):
+    n = mesh.shape["mp"]
+    paired = mesh.shape["seq"] == 2 and mesh.shape["dp"] == 4
     return jax.shard_map(
-        shards,
+        functools.partial(shards, n) if paired else plain_shards,
         mesh=mesh,
         in_specs=(
             P(("dp", "seq", "mp"), None),

time: 275 us -> 186 us (0.68)
  the two profiles are of different devices: /device:TPU:0 before, /device:TPU:9 now
where the time goes in v1:
time: 186 us
  Pallas kernels  170 us (91%)
  other arithmetic  9.89 us (5%)
  local copies, waits for them, and re-layouts  5.19 us (3%)
    pallas_call x1, Pallas kernels, shards(): pl.pallas_call(functools.partial(kernel, n), out_shape=(jax.ShapeDtypeStr...  170 us

profile of v1, /device:TPU:9, one launch (start us, length us, event | category | flops | bytes accessed | tf_op | source)
XLA Modules:
  0.0 185.7 jit_solution(5261973030923185564)
XLA Ops:
  0.6 0.0 copy-start
  0.6 0.0 copy-start.3
  0.7 0.0 copy-start.4
  0.7 0.0 copy-start.1
  0.7 0.8 convert_element_type.31
  1.5 1.1 convert_reduce_fusion
  2.6 1.3 fusion.2
  3.9 1.1 multiply_convert_fusion
  5.1 0.8 pad.12.masked_ref
  5.8 0.0 copy-done
  5.8 0.0 copy-done.3
  5.8 0.0 copy-done.4
  5.9 1.1 fusion.5.normed_ref
  6.9 0.8 pad.11.x_ref
  7.7 0.0 copy-done.1
  7.7 0.3 reshape.33
  8.1 1.4 pad.13.h_ref
  9.4 169.9 %mlp_backward.1 = (bf16[208,1024]{1,0:T(8,128)(2,1)}, bf16[2,2,128,1024]{3,2,1,0:T(8,128)(2,1)}, bf16[2,2,256,512]{3,2,1,0:T(8,128)(2,1)}) custom-call(bf16[208,1024]{1,0:T(8,128)(2,1)} %pad.11.x_ref, bf16[208,1024]{1,0:T(8,128)(2,1)} %fusion.5.normed_ref, bf16[208,1024]{1,0:T(8,128)(2,1)} %pad.12.masked_ref, bf16[4,208,1024]{2,1,0:T(8,128)(2,1)} %pad.13.h_ref, ...), custom_call_target="tpu_custom_call" | custom-call | tf_op jit(solution)/shard_map/mlp_backward/pallas_call | solution.py:329
  179.4 0.0 copy-start.2
  179.4 1.9 %slice.3 = bf16[196,1024]{1,0:T(8,128)(2,1)} slice(bf16[208,1024]{1,0:T(8,128)(2,1)} %get-tuple-element.6), slice={[0:196], [0:1024]} | slice | bytes 802816 | tf_op jit(solution)/shard_map/slice | solution.py:346
  181.3 2.8 %convert_multiply_fusion.1 = f32[2,2,128,1024]{3,2,1,0:T(8,128)} fusion(bf16[2,2,128,1024]{3,2,1,0:T(8,128)(2,1)} %get-tuple-element.7), kind=kLoop, calls=%fused_computation.1 | loop fusion | flops 1048576 | bytes 3145728 | tf_op jit(solution)/shard_map/mul | solution.py:347
  184.1 0.0 copy-done.2
  184.1 1.6 convert_multiply_fusion
  (2 shorter events, 0.0 us)
Async XLA Ops:
  0.6 5.2 %copy-start = (bf16[196,1024]{1,0:T(8,128)(2,1)S(1)}, bf16[196,1024]{1,0:T(8,128)(2,1)}, u32[]{:S(2)}) copy-start(bf16[196,1024]{1,0:T(8,128)(2,1)} %param.8) | copy-start | bytes 1204228
  0.6 5.2 %copy-start.3 = (f32[1024]{0:T(1024)S(1)}, f32[1024]{0:T(1024)}, u32[]{:S(2)}) copy-start(f32[1024]{0:T(1024)} %param.14) | copy-start | bytes 12292
  0.7 5.2 %copy-start.4 = (f32[1024]{0:T(1024)S(1)}, f32[1024]{0:T(1024)}, u32[]{:S(2)}) copy-start(f32[1024]{0:T(1024)} %param.15) | copy-start | bytes 12292
  0.7 7.1 %copy-start.1 = (bf16[784,1024]{1,0:T(8,128)(2,1)S(1)}, bf16[784,1024]{1,0:T(8,128)(2,1)}, u32[]{:S(2)}) copy-start(bf16[784,1024]{1,0:T(8,128)(2,1)} %param.11) | copy-start | bytes 4816900
  179.4 4.7 %copy-start.2 = (bf16[2,2,256,512]{3,2,1,0:T(8,128)(2,1)S(1)}, bf16[2,2,256,512]{3,2,1,0:T(8,128)(2,1)}, u32[]{:S(2)}) copy-start(bf16[2,2,256,512]{3,2,1,0:T(8,128)(2,1)} %get-tuple-element.8) | copy-start | bytes 3145732

commit v2 on v1

--- a/solution.py
+++ b/solution.py
@@ -134,23 +134,25 @@
             send_sem=r_send.at[d, j], recv_sem=r_recv.at[d, j],
             device_id={"mp": peer[d]}, device_id_type=MESH)
 
-    def running(j):
-        for d in (0, 1):
+    def line_step(d, k):
+        return k - z if d == 0 else k - (n - 1 - z)
+
+    def running(k):
+        for d in (0, 1):
+            j = line_step(d, k)
             t = n - 1 - j if d == 0 else j
-            beyond = z < t if d == 0 else z > t
-            gets = jnp.logical_and(has[1 - d], z <= t if d == 0 else z >= t)
+            gets = jnp.logical_and(has[1 - d], j >= 0)
 
             @pl.when(gets)
             def _(d=d, t=t, j=j):
                 run_copy(d, j).wait_recv()
-
-            @pl.when(jnp.logical_and(gets, beyond))
-            def _(d=d, t=t, j=j):
-                dn[t] = (dn[t].astype(F32) + slots[d][t].astype(F32)).astype(BF)
-
-            @pl.when(beyond)
-            def _(d=d, t=t, j=j):
-                run_copy(d, j).start()
+                if k < n - 1:
+                    dn[t] = (dn[t].astype(F32) + slots[d][t].astype(F32)).astype(BF)
+
+            if k < n - 1:
+                @pl.when(j >= 0)
+                def _(d=d, j=j):
+                    run_copy(d, j).start()
 
     def grad_parts(which):
         return ((t_in, rc_in, ry_in, rx_in, out_in), (t_out, rc_out, ry_out, rx_out, out_out))[which]
@@ -222,6 +224,7 @@
             d_copy(which, 3, c).start()
 
     stages = [after_core, after_seq, after_chip]
+    running(0)
     make_out()
     stages.pop(0)(1)
     for s in range(1, n):
@@ -233,7 +236,8 @@
             @pl.when(forwards(d, s))
             def _(d=d):
                 n_copy(d, s).start()
-        running(s - 1)
+        if s < n - 1:
+            running(s)
         if stages:
             stages.pop(0)(1)
     for stage in stages:
@@ -289,11 +293,11 @@
             def _(d=d, s=s):
                 m_copy(d, s).wait_send()
                 n_copy(d, s).wait_send()
-    for j in range(n):
-        for d in (0, 1):
-            t = n - 1 - j if d == 0 else j
-
-            @pl.when(z < t if d == 0 else z > t)
+    for k in range(n - 1):
+        for d in (0, 1):
+            j = line_step(d, k)
+
+            @pl.when(j >= 0)
             def _(d=d, j=j):
                 run_copy(d, j).wait_send()
 

time: 186 us -> 116 us (0.62)
  the two profiles are of different devices: /device:TPU:9 before, /device:TPU:0 now
where the time goes in v2:
time: 116 us
  Pallas kernels  99.9 us (86%)
  other arithmetic  9.89 us (9%)
  local copies, waits for them, and re-layouts  5.19 us (4%)
    pallas_call x1, Pallas kernels, shards(): pl.pallas_call(functools.partial(kernel, n), out_shape=(jax.ShapeDtypeStr...  99.9 us
    mul x1, other arithmetic, shards(): g_in.reshape(width // 2, ff).astype(F32) * scale  2.83 us

profile of v2, /device:TPU:0, one launch (start us, length us, event | category | flops | bytes accessed | tf_op | source)
XLA Modules:
  0.0 115.7 jit_solution(8701627135960301679)
XLA Ops:
  0.6 0.0 copy-start
  0.6 0.0 copy-start.3
  0.7 0.0 copy-start.4
  0.7 0.0 copy-start.1
  0.7 0.8 convert_element_type.31
  1.5 1.1 convert_reduce_fusion
  2.6 1.3 %fusion.2 = f32[208]{0:T(256)S(1)} fusion(f32[208]{0:T(256)S(1)} %broadcast_multiply_fusion, bf16[196,1024]{1,0:T(8,128)(2,1)} %param.8), kind=kLoop, calls=%fused_computation.6 | loop fusion | flops 851760 | bytes 403072 | tf_op jit(solution)/shard_map/reduce_sum | solution.py:314
  3.9 1.1 multiply_convert_fusion
  5.1 0.8 pad.12.masked_ref
  5.8 0.0 copy-done
  5.8 0.0 copy-done.3
  5.8 0.0 copy-done.4
  5.9 1.1 fusion.5.normed_ref
  6.9 0.8 pad.11.x_ref
  7.7 0.0 copy-done.1
  7.7 0.3 reshape.33
  8.1 1.4 %pad.13.h_ref = bf16[4,208,1024]{2,1,0:T(8,128)(2,1)} pad(bf16[4,196,1024]{2,1,0:T(8,128)(2,1)S(1)} %reshape.33, bf16[]{:T(256)} %constant.5.clone.1), padding=0_0x0_12x0_0 | pad | bytes 3309570 | tf_op jit(solution)/shard_map/jit(_pad)/pad | solution.py:318
  9.4 99.9 %mlp_backward.1 = (bf16[208,1024]{1,0:T(8,128)(2,1)}, bf16[2,2,128,1024]{3,2,1,0:T(8,128)(2,1)}, bf16[2,2,256,512]{3,2,1,0:T(8,128)(2,1)}) custom-call(bf16[208,1024]{1,0:T(8,128)(2,1)} %pad.11.x_ref, bf16[208,1024]{1,0:T(8,128)(2,1)} %fusion.5.normed_ref, bf16[208,1024]{1,0:T(8,128)(2,1)} %pad.12.masked_ref, bf16[4,208,1024]{2,1,0:T(8,128)(2,1)} %pad.13.h_ref, ...), custom_call_target="tpu_custom_call" | custom-call | tf_op jit(solution)/shard_map/mlp_backward/pallas_call | solution.py:333
  109.3 0.0 copy-start.2
  109.3 1.9 %slice.3 = bf16[196,1024]{1,0:T(8,128)(2,1)} slice(bf16[208,1024]{1,0:T(8,128)(2,1)} %get-tuple-element.6), slice={[0:196], [0:1024]} | slice | bytes 802816 | tf_op jit(solution)/shard_map/slice | solution.py:350
  111.2 2.8 %convert_multiply_fusion.1 = f32[2,2,128,1024]{3,2,1,0:T(8,128)} fusion(bf16[2,2,128,1024]{3,2,1,0:T(8,128)(2,1)} %get-tuple-element.7), kind=kLoop, calls=%fused_computation.1 | loop fusion | flops 1048576 | bytes 3145728 | tf_op jit(solution)/shard_map/mul | solution.py:351
  114.0 0.0 copy-done.2
  114.0 1.6 %convert_multiply_fusion = f32[2,2,256,512]{3,2,1,0:T(8,128)} fusion(bf16[2,2,256,512]{3,2,1,0:T(8,128)(2,1)S(1)} %copy-done.2), kind=kLoop, calls=%fused_computation | loop fusion | flops 1048576 | bytes 3145728 | tf_op jit(solution)/shard_map/mul | solution.py:352
  (2 shorter events, 0.0 us)
Async XLA Ops:
  0.6 5.2 %copy-start = (bf16[196,1024]{1,0:T(8,128)(2,1)S(1)}, bf16[196,1024]{1,0:T(8,128)(2,1)}, u32[]{:S(2)}) copy-start(bf16[196,1024]{1,0:T(8,128)(2,1)} %param.8) | copy-start | bytes 1204228
  0.6 5.2 %copy-start.3 = (f32[1024]{0:T(1024)S(1)}, f32[1024]{0:T(1024)}, u32[]{:S(2)}) copy-start(f32[1024]{0:T(1024)} %param.14) | copy-start | bytes 12292
  0.7 5.2 %copy-start.4 = (f32[1024]{0:T(1024)S(1)}, f32[1024]{0:T(1024)}, u32[]{:S(2)}) copy-start(f32[1024]{0:T(1024)} %param.15) | copy-start | bytes 12292
  0.7 7.1 %copy-start.1 = (bf16[784,1024]{1,0:T(8,128)(2,1)S(1)}, bf16[784,1024]{1,0:T(8,128)(2,1)}, u32[]{:S(2)}) copy-start(bf16[784,1024]{1,0:T(8,128)(2,1)} %param.11) | copy-start | bytes 4816900
  109.3 4.7 %copy-start.2 = (bf16[2,2,256,512]{3,2,1,0:T(8,128)(2,1)S(1)}, bf16[2,2,256,512]{3,2,1,0:T(8,128)(2,1)}, u32[]{:S(2)}) copy-start(bf16[2,2,256,512]{3,2,1,0:T(8,128)(2,1)} %get-tuple-element.8) | copy-start | bytes 3145732
